TPU v7x, 32 devices: a whole 2x2x4 slice. The times are simulated.
32 devices in a mesh: seq: 16 (over z, y, core), head: 2 (over x).
Axes of the slice: x: 2, y: 2, z: 4, core: 2. Of those that a mesh axis runs over, the one named last changes fastest.
Arguments:
- teacher: bfloat16 [1, 4096, 4096], P(None, 'seq', 'head'), may hold values from -32 to 32
- student: bfloat16 [1, 4096, 1792], P(None, 'seq', 'head'), may hold values from -32 to 32
- weights: float32 [4096], P('seq'), may hold values from 1 to 32
Outputs:
- mean_loss: float32 [], replicated
- student_grad: float32 [1, 4096, 1792], P(None, 'seq', 'head')
All inputs are finite; a program needn't handle non-finite values.
Results may differ from a plain program's by a relative error of at most 0.0011.
Values may be sent and summed in bfloat16 or wider, within the bound.
A program may use at most 128 MiB of HBM per device.

v0:
```python
import math

import jax
import jax.numpy as jnp
from jax import lax
from jax.sharding import PartitionSpec as P

TW = 256
SW = 112
HEADS = 16


def relation_scores(own_rows, key_piece, head_size):
    relations, tok_rows, columns = own_rows.shape
    head_count = columns // head_size
    queries = own_rows.reshape(relations, tok_rows, head_count, head_size)
    keys_split = key_piece.reshape(relations, key_piece.shape[1], head_count, head_size)
    return jnp.einsum(
        "rihd,rjhd->rhij", queries, keys_split, preferred_element_type=jnp.float32
    ) * (1.0 / math.sqrt(head_size))


def local(teacher, student, weights):
    relations, tok_rows, columns = teacher.shape
    head_count = columns // TW
    cycle_size = lax.axis_size("seq")
    lowest = jnp.full((relations, head_count, tok_rows), -jnp.inf, jnp.float32)
    zeroes = jnp.zeros((relations, head_count, tok_rows), jnp.float32)
    pieces = (
        lax.all_gather(teacher, "seq", axis=1, tiled=True),
        lax.all_gather(student, "seq", axis=1, tiled=True),
    )
    teach_max = lowest
    teach_sum = zeroes
    teach_cross = zeroes
    stud_max = lowest
    stud_sum = zeroes
    teach_score = relation_scores(teacher, pieces[0], TW)
    stud_score = relation_scores(student, pieces[1], SW)
    teach_top = jnp.max(teach_score, axis=-1)
    stud_top = jnp.max(stud_score, axis=-1)
    teach_exp = jnp.exp(teach_score - teach_top[..., None])
    stud_exp = jnp.exp(stud_score - stud_top[..., None])
    teach_keep = jnp.exp(teach_max - teach_top)
    stud_keep = jnp.exp(stud_max - stud_top)
    sweep_stats = (
        teach_top,
        teach_sum * teach_keep + jnp.sum(teach_exp, axis=-1),
        teach_cross * teach_keep + jnp.sum(teach_exp * (teach_score - stud_score), axis=-1),
        stud_top,
        stud_sum * stud_keep + jnp.sum(stud_exp, axis=-1),
    )
    teach_max, teach_sum, teach_cross, stud_max, stud_sum = sweep_stats
    teach_norm = teach_max + jnp.log(teach_sum)
    stud_norm = stud_max + jnp.log(stud_sum)
    divergence = teach_cross / teach_sum - teach_norm + stud_norm
    partial_loss = jnp.sum(weights[None, None, :] * divergence)
    loss_sum = lax.psum(partial_loss, ("seq", "head"))
    mean_loss = loss_sum / (relations * HEADS * tok_rows * cycle_size)
    every_teach, every_stud, every_weight = (
        lax.all_gather(teach_norm, "seq", axis=2, tiled=True),
        lax.all_gather(stud_norm, "seq", axis=2, tiled=True),
        lax.all_gather(weights, "seq", axis=0, tiled=True),
    )
    pieces = (
        lax.all_gather(teacher, "seq", axis=1, tiled=True),
        lax.all_gather(student, "seq", axis=1, tiled=True),
    )
    key_count = pieces[0].shape[1]
    teach_score = relation_scores(teacher, pieces[0], TW)
    stud_score = relation_scores(student, pieces[1], SW)
    row_part = weights[None, None, :, None] * (
        jnp.exp(stud_score - stud_norm[..., None]) - jnp.exp(teach_score - teach_norm[..., None])
    )
    col_part = every_weight[None, None, None, :] * (
        jnp.exp(stud_score - every_stud[:, :, None, :])
        - jnp.exp(teach_score - every_teach[:, :, None, :])
    )
    slope_mix = (row_part + col_part).astype(jnp.bfloat16)
    stud_keys = pieces[1].reshape(relations, key_count, head_count, SW)
    summed = jnp.einsum("rhij,rjhd->rihd", slope_mix, stud_keys, preferred_element_type=jnp.float32)
    student_grad = (summed * (1.0 / math.sqrt(SW))).reshape(relations, tok_rows, head_count * SW)
    return (mean_loss, student_grad)


def solution(mesh):
    return jax.shard_map(
        local,
        mesh=mesh,
        in_specs=(P(None, "seq", "head"), P(None, "seq", "head"), P("seq")),
        out_specs=(P(), P(None, "seq", "head")),
        check_vma=False,
    )
```

profile of v0, /device:TPU:24, one launch (start us, length us, event | category | flops | bytes accessed | tf_op | source)
XLA Modules:
  0.0 387.1 jit_solution(11814815298845756084)
XLA Ops:
  7.2 0.0 all-gather.6.cloned.1.call-start
  7.2 0.7 all-gather.6.cloned.1.call-update
  7.9 0.0 all-gather.4.cloned.1.call-start
  7.9 2.3 copy.15
  10.2 0.0 all-gather.4.cloned.1.call-update
  10.2 1.2 copy.18
  11.5 1.5 copy.22
  13.0 17.5 %all-gather = f32[16,1,256]{2,1,0:T(1,128)S(1)} all-gather(f32[1,1,256]{2,1,0:T(1,128)} %bitcast.61), channel_id=1, replica_groups=mesh['seq'=16,'head'=2] {'seq'}, dimensions={0}, use_global_device_ids=true | all-gather | bytes 17408 | tf_op jit(solution)/shard_map/all_gather | solution.py:63
  30.5 47.2 %all-gather.6.cloned.1.call-done = bf16[1,4096,896]{2,1,0:T(8,128)(2,1)} async-done(((bf16[1,256,896]{2,1,0:T(8,128)(2,1)}), bf16[1,4096,896]{2,1,0:T(8,128)(2,1)}) %all-gather.6.cloned.1.call-update) | async-done | bytes 7340048 | tf_op jit(solution)/shard_map/all_gather | solution.py:31
  77.7 10.7 %copy.19 = bf16[1,4096,896]{1,2,0:T(8,128)(2,1)} copy(bf16[1,4096,896]{2,1,0:T(8,128)(2,1)} %all-gather.6.cloned.1.call-done) | data formatting | bytes 14680064 | tf_op jit(solution)/shard_map/all_gather | solution.py:31
  88.5 119.5 %all-gather.4.cloned.1.call-done = bf16[1,4096,2048]{1,2,0:T(8,128)(2,1)} async-done(((bf16[1,256,2048]{1,2,0:T(8,128)(2,1)}), bf16[1,4096,2048]{1,2,0:T(8,128)(2,1)}) %all-gather.4.cloned.1.call-update) | async-done | bytes 16777232 | tf_op jit(solution)/shard_map/all_gather | solution.py:30
  207.9 19.3 %multiply_reduce_fusion.2 = (f32[8,256]{1,0:T(8,128)S(1)}, f32[8,256,4096]{2,1,0:T(8,128)}) fusion(bf16[4096,8,256]{0,2,1:T(8,128)(2,1)} %bitcast.51, bf16[256,8,256]{2,1,0:T(8,128)(2,1)S(1)} %bitcast.54), kind=kOutput, calls=%fused_computation.6 | convolution fusion | flops 4311742464 | bytes 51388416 | tf_op jit(solution)/shard_map/rihd,rjhd->rhij/dot_general | solution.py:18
  227.2 29.6 %fusion = (f32[8,256]{1,0:T(8,128)S(1)}, f32[8,256]{1,0:T(8,128)S(1)}, f32[8,256]{1,0:T(8,128)S(1)}, f32[8,256,4096]{2,1,0:T(8,128)}) fusion(f32[8,256,4096]{2,1,0:T(8,128)} %get-tuple-element.15, f32[8,256]{1,0:T(8,128)S(1)} %get-tuple-element.14, bf16[256,8,112]{0,2,1:T(8,128)(2,1)S(1)} %bitcast.57, bf16[4096,8,112]{0,2,1:T(8,128)(2,1)} %bitcast.52), kind=kOutput, calls=%fused_computation.4 | convolution fusion | flops 1946150912 | bytes 74940416 | tf_op jit(solution)/shard_map/rihd,rjhd->rhij/dot_general | solution.py:18
  256.8 0.0 copy-start
  256.8 14.0 %exponential_reduce_fusion = f32[8,256]{1,0:T(8,128)S(1)} fusion(f32[8,256,4096]{2,1,0:T(8,128)} %get-tuple-element.16, f32[8,256]{1,0:T(8,128)S(1)} %get-tuple-element.10), kind=kLoop, calls=%fused_computation.1 | loop fusion | flops 25163776 | bytes 33570816 | tf_op jit(solution)/shard_map/reduce_sum | solution.py:51
  270.9 0.0 copy-done
  270.9 0.6 multiply_reduce_fusion.3
  271.5 39.4 %psum.7 = f32[]{:T(128)} all-reduce(f32[]{:T(128)} %get-tuple-element.11), channel_id=1, replica_groups=mesh['seq'=16,'head'=2] {'seq','head'}, use_global_device_ids=true, to_apply=%region_6.0 | all-reduce | flops 1 | bytes 8 | tf_op jit(solution)/shard_map/psum | solution.py:58
  310.9 18.1 %all_gather.21 = f32[1,8,4096]{2,1,0:T(8,128)S(1)} all-gather(f32[1,8,256]{2,1,0:T(8,128)S(1)} %fusion.6), channel_id=1, replica_groups=mesh['seq'=16,'head'=2] {'seq'}, dimensions={2}, use_global_device_ids=true | all-gather | bytes 139264 | tf_op jit(solution)/shard_map/all_gather | solution.py:61
  329.0 18.8 %all_gather.20 = f32[1,8,4096]{2,1,0:T(8,128)S(1)} all-gather(f32[1,8,256]{2,1,0:T(8,128)S(1)} %fusion.10), channel_id=1, replica_groups=mesh['seq'=16,'head'=2] {'seq'}, dimensions={2}, use_global_device_ids=true | all-gather | bytes 139264 | tf_op jit(solution)/shard_map/all_gather | solution.py:62
  347.8 29.4 %fusion.2 = f32[8,256,112]{1,2,0:T(8,128)S(1)} fusion(bf16[4096,8,112]{0,2,1:T(8,128)(2,1)} %bitcast.53, f32[8,256,4096]{2,1,0:T(8,128)} %get-tuple-element.16, f32[8,256,4096]{2,1,0:T(8,128)} %get-tuple-element.15, f32[8,4096]{1,0:T(8,128)S(1)} %bitcast.58, f32[8,4096]{1,0:T(8,128)S(1)} %bitcast.59, f32[4096]{0:T(1024)S(1)} %bitcast.60, ...), kind=kOutput, calls=%fused_computation.8 | convolution fusion | flops 1979940864 | bytes 75662336 | tf_op jit(solution)/shard_map/rhij,rjhd->rihd/dot_general | solution.py:81
  377.2 1.2 copy.20
  (2 shorter events, 0.0 us)
Async XLA Ops:
  7.2 70.6 %all-gather.6.cloned.1.call-start = ((), (), s32[]{:S(2)}) async-start(), calls=%async_computation.1 | async-start | bytes 7798784 | tf_op jit(solution)/shard_map/all_gather | solution.py:31
  7.9 200.0 %all-gather.4.cloned.1.call-start = ((), (), s32[]{:S(2)}) async-start(), calls=%async_computation | async-start | bytes 17825792 | tf_op jit(solution)/shard_map/all_gather | solution.py:30
  256.8 14.1 %copy-start = (f32[256]{0:T(256)S(1)}, f32[256]{0:T(256)}, u32[]{:S(2)}) copy-start(f32[256]{0:T(256)} %param.5) | copy-start | bytes 3076
Sparse Core Ops, SparseCore 0:
  10.3 67.4 all-gather.5
  79.9 127.9 all-gather.3
where the time goes:
time: 393 us; the launch traced here: 387 us
  waiting for transfers between devices  167 us (42%)
  blocking collectives  93.8 us (24%)
  matrix products  78.3 us (20%)
  local copies, waits for them, and re-layouts  17 us (4%)
  between operations  15.9 us (4%)
  other arithmetic  14.7 us (4%)
    all_gather x1, waiting for transfers between devices, local(): lax.all_gather(teacher, 'seq', axis=1, tiled=True)  119 us
    dot_general x2, matrix products, relation_scores(): jnp.einsum('rihd,rjhd->rhij', queries, keys_split, preferred_element_type...  48.9 us
    all_gather x1, waiting for transfers between devices, local(): lax.all_gather(student, 'seq', axis=1, tiled=True)  47.2 us
    psum x1, blocking collectives, local(): loss_sum = lax.psum(partial_loss, ('seq', 'head'))  39.4 us
    dot_general x1, matrix products, local(): jnp.einsum('rhij,rjhd->rihd', slope_mix, stud_keys, preferred_element_typ...  29.4 us
    all_gather x1, blocking collectives, local(): lax.all_gather(stud_norm, 'seq', axis=2, tiled=True)  18.8 us
    all_gather x1, blocking collectives, local(): lax.all_gather(teach_norm, 'seq', axis=2, tiled=True)  18.1 us
    all_gather x1, blocking collectives, local(): lax.all_gather(weights, 'seq', axis=0, tiled=True)  17.5 us
  transfers between devices with their start and end apart: 2, of which 2 were waited for; matrix products, arithmetic and copies ran while one was open for 4% of the time, Pallas kernels for 0%

commit v1 on v0

v1 whole, which is shorter than its diff:
```python
import functools
import math

import jax
import jax.numpy as jnp
from jax import lax
from jax.experimental import pallas as pl
from jax.experimental.pallas import tpu as pltpu
from jax.sharding import PartitionSpec as P

TW = 256
SW = 112
LANES = 128
LOG2E = math.log2(math.e)
LN2 = math.log(2.0)
NT = (((1,), (1,)), ((), ()))


def dot_nt(a, b):
    return lax.dot_general(a, b, NT, preferred_element_type=jnp.float32)


def kernel(
    heads, group, unroll, t_in, u_in, w_in, grad_out, loss_out,
    t_all, u_all, w_all, norms, grads,
    t_send, u_send, w_send, t_fwd, u_fwd, t_recv, u_recv, w_recv, n_send, n_recv, g_send, g_recv,
):
    n = heads * group
    block = t_in.shape[0]
    me = lax.axis_index("seq")
    head = lax.div(me, group)
    member = lax.rem(me, group)
    t_scale = LOG2E / math.sqrt(TW)
    u_scale = LOG2E / math.sqrt(SW)

    def other_head(i):
        return lax.rem(head + i, heads)

    def other_member(i):
        return lax.rem(member + i, group)

    def remote(src, dst, send, recv, device):
        return pltpu.make_async_remote_copy(
            src_ref=src, dst_ref=dst, send_sem=send, recv_sem=recv,
            device_id={"seq": device}, device_id_type=pl.DeviceIdType.MESH,
        )

    def rows(slot):
        return pl.ds(pl.multiple_of(slot * block, block), block)

    def columns(h):
        return pl.ds(pl.multiple_of(h * TW, TW), TW)

    barrier = pltpu.get_barrier_semaphore()
    for i in range(1, heads):
        pl.semaphore_signal(barrier, inc=1, device_id={"seq": other_head(i) * group + member}, device_id_type=pl.DeviceIdType.MESH)
    for i in range(1, group):
        pl.semaphore_signal(barrier, inc=1, device_id={"seq": head * group + other_member(i)}, device_id_type=pl.DeviceIdType.MESH)
    pl.semaphore_wait(barrier, heads + group - 2)

    direct = []
    for i in range(1, heads):
        h = other_head(i)
        device = h * group + member
        direct += [
            remote(t_in.at[:, columns(h)], t_all.at[rows(me)], t_send.at[i], t_recv.at[me], device),
            remote(u_in.at[h], u_all.at[rows(me)], u_send.at[i], u_recv.at[me], device),
            remote(w_in, w_all.at[head], w_send.at[i], w_recv.at[head], device),
        ]
    for copy in direct:
        copy.start()
    forwards = []

    def forward(i, slot, t_src, u_src):
        for g in range(1, group):
            device = head * group + other_member(g)
            pair = [
                remote(t_src, t_all.at[rows(slot)], t_fwd.at[i, g], t_recv.at[slot], device),
                remote(u_src, u_all.at[rows(slot)], u_fwd.at[i, g], u_recv.at[slot], device),
            ]
            for copy in pair:
                copy.start()
            forwards.extend(pair)

    def arrived(slot):
        remote(t_in.at[:, columns(0)], t_all.at[rows(slot)], t_send.at[0], t_recv.at[slot], me).wait_recv()
        remote(u_in.at[0], u_all.at[rows(slot)], u_send.at[0], u_recv.at[slot], me).wait_recv()

    forward(0, me, t_in.at[:, columns(head)], u_in.at[head])
    t_all[rows(me), :] = t_in[:, columns(head)]
    u_all[rows(me), :] = u_in[head]
    w_all[head] = w_in[...]
    for i in range(1, heads):
        h = lax.rem(head + heads - i, heads)
        slot = h * group + member
        arrived(slot)
        forward(i, slot, t_all.at[rows(slot)], u_all.at[rows(slot)])
        remote(w_in, w_all.at[h], w_send.at[0], w_recv.at[h], me).wait_recv()
    for i in range(heads):
        for g in range(1, group):
            h = lax.rem(head + heads - i, heads)
            arrived(h * group + other_member(g))

    def row_stats(i, loss):
        slot = i * group + member
        t_own = t_all[rows(slot), :]
        u_own = u_all[rows(slot), :]

        def step(j, state):
            for q in range(unroll):
                t_max, t_sum, t_cross, u_max, u_sum = state
                keys = rows(j * unroll + q)
                t_score = (dot_nt(t_all[keys, :], t_own) * t_scale).reshape(block // 8, 8, block)
                u_score = (dot_nt(u_all[keys, :], u_own) * u_scale).reshape(block // 8, 8, block)
                t_top = jnp.maximum(t_max, jnp.max(t_score, axis=0))
                u_top = jnp.maximum(u_max, jnp.max(u_score, axis=0))
                t_exp = jnp.exp2(t_score - t_top[None])
                u_exp = jnp.exp2(u_score - u_top[None])
                t_keep = jnp.exp2(t_max - t_top)
                u_keep = jnp.exp2(u_max - u_top)
                state = (
                    t_top,
                    t_sum * t_keep + jnp.sum(t_exp, axis=0),
                    t_cross * t_keep + jnp.sum(t_exp * (t_score - u_score), axis=0),
                    u_top,
                    u_sum * u_keep + jnp.sum(u_exp, axis=0),
                )
            return state

        low = jnp.full((8, block), -1e30, jnp.float32)
        zero = jnp.zeros((8, block), jnp.float32)
        t_max, t_sum, t_cross, u_max, u_sum = lax.fori_loop(0, n // unroll, step, (low, zero, zero, low, zero))
        t_top = jnp.max(t_max, axis=0, keepdims=True)
        u_top = jnp.max(u_max, axis=0, keepdims=True)
        t_keep = jnp.exp2(t_max - t_top)
        t_total = jnp.sum(t_sum * t_keep, axis=0, keepdims=True)
        t_mixed = jnp.sum(t_cross * t_keep, axis=0, keepdims=True)
        u_total = jnp.sum(u_sum * jnp.exp2(u_max - u_top), axis=0, keepdims=True)
        t_norm = t_top + jnp.log(t_total) * LOG2E
        u_norm = u_top + jnp.log(u_total) * LOG2E
        weight = w_all[i][:1, :]
        weight_log = jnp.log(weight) * LOG2E
        norms[member, i, 0:8, :] = jnp.broadcast_to(t_norm - weight_log, (8, block))
        norms[member, i, 8:16, :] = jnp.broadcast_to(u_norm - weight_log, (8, block))
        return loss + weight * (t_mixed / t_total - t_norm + u_norm)

    loss = lax.fori_loop(0, heads, row_stats, jnp.zeros((1, block), jnp.float32))
    stats = [
        remote(norms.at[member], norms.at[member], n_send.at[g], n_recv.at[member], head * group + other_member(g))
        for g in range(1, group)
    ]
    for copy in stats:
        copy.start()
    loss_out[...] = jnp.broadcast_to(loss * LN2, loss_out.shape)
    for g in range(1, group):
        m = other_member(g)
        remote(norms.at[m], norms.at[m], n_send.at[0], n_recv.at[m], me).wait_recv()

    def row_grad(i):
        slot = i * group + member
        t_own = t_all[rows(slot), :]
        u_own = u_all[rows(slot), :]

        def own_norm(first):
            tall = jnp.broadcast_to(norms[member, i, first:first + 1, :], (LANES, block)).T
            return jnp.concatenate([tall] * (block // LANES), axis=1)

        t_mine = own_norm(0)
        u_mine = own_norm(8)

        def step(j, total):
            for q in range(unroll):
                key = j * unroll + q
                keys = rows(key)
                key_head = lax.div(key, group)
                key_member = lax.rem(key, group)
                t_theirs = norms[key_member, key_head, 0:1, :]
                u_theirs = norms[key_member, key_head, 8:9, :]
                u_keys = u_all[keys, :]
                t_score = dot_nt(t_own, t_all[keys, :]) * t_scale
                u_score = dot_nt(u_own, u_keys) * u_scale
                row_part = jnp.exp2(u_score - u_mine) - jnp.exp2(t_score - t_mine)
                col_part = jnp.exp2(u_score - u_theirs) - jnp.exp2(t_score - t_theirs)
                mix = (row_part + col_part).astype(jnp.bfloat16)
                total = total + jnp.dot(mix, u_keys, preferred_element_type=jnp.float32)
            return total

        total = lax.fori_loop(0, n // unroll, step, jnp.zeros((block, LANES), jnp.float32))
        return total * (1.0 / math.sqrt(SW))

    def send_grad(i, h):
        return remote(grads.at[h], grad_out.at[head], g_send.at[h], g_recv.at[head], h * group + member)

    def grad_step(i, carry):
        h = other_head(i)
        grads[h] = row_grad(h)
        send_grad(i, h).start()
        return carry

    lax.fori_loop(1, heads, grad_step, 0)
    grad_out[head] = row_grad(head)

    for copy in direct + forwards + stats:
        copy.wait_send()
    for i in range(1, heads):
        h = other_head(i)
        send_grad(i, h).wait_send()
        remote(grads.at[h], grad_out.at[h], g_send.at[h], g_recv.at[h], me).wait_recv()


def local(teacher, student, weights):
    relations, block, t_columns = teacher.shape
    assert relations == 1
    heads = t_columns // TW
    n = lax.axis_size("seq")
    assert n % heads == 0
    group = n // heads
    unroll = math.gcd(n, 4)
    u_in = student.reshape(block, heads, SW).transpose(1, 0, 2)
    u_in = jnp.pad(u_in, ((0, 0), (0, 0), (0, LANES - SW)))
    w_in = jnp.broadcast_to(weights[None, :], (8, block))
    vmem = pl.BlockSpec(memory_space=pltpu.VMEM)
    dma = pltpu.SemaphoreType.DMA
    grads, loss = pl.pallas_call(
        functools.partial(kernel, heads, group, unroll),
        out_shape=(
            jax.ShapeDtypeStruct((heads, block, LANES), jnp.float32),
            jax.ShapeDtypeStruct((8, block), jnp.float32),
        ),
        in_specs=[vmem] * 3,
        out_specs=(vmem, vmem),
        scratch_shapes=[
            pltpu.VMEM((n * block, TW), jnp.bfloat16),
            pltpu.VMEM((n * block, LANES), jnp.bfloat16),
            pltpu.VMEM((heads, 8, block), jnp.float32),
            pltpu.VMEM((group, heads, 16, block), jnp.float32),
            pltpu.VMEM((heads, block, LANES), jnp.float32),
            dma((heads,)), dma((heads,)), dma((heads,)),
            dma((heads, group)), dma((heads, group)),
            dma((n,)), dma((n,)), dma((heads,)),
            dma((group,)), dma((group,)),
            dma((heads,)), dma((heads,)),
        ],
        compiler_params=pltpu.CompilerParams(
            collective_id=0, has_side_effects=True, vmem_limit_bytes=60 * 2**20
        ),
    )(teacher[0], u_in, w_in)
    total = lax.psum(jnp.sum(loss[0]), ("seq", "head"))
    mean_loss = total / (heads * lax.axis_size("head") * block * n)
    student_grad = grads[:, :, :SW].transpose(1, 0, 2).reshape(1, block, heads * SW)
    return (mean_loss, student_grad)


def solution(mesh):
    return jax.shard_map(
        local,
        mesh=mesh,
        in_specs=(P(None, "seq", "head"), P(None, "seq", "head"), P("seq")),
        out_specs=(P(), P(None, "seq", "head")),
        check_vma=False,
    )
```

time: 393 us -> 163 us (0.41)
  the two profiles are of different devices: /device:TPU:24 before, /device:TPU:0 now
where the time goes in v1:
time: 163 us
  Pallas kernels  107 us (66%)
  blocking collectives  45.5 us (28%)
  local copies, waits for them, and re-layouts  6.51 us (4%)
  between operations  2.46 us (2%)
    pallas_call x1, Pallas kernels, local(): pl.pallas_call(functools.partial(kernel, heads, group, unroll), out_shape...  107 us
    psum x1, blocking collectives, local(): total = lax.psum(jnp.sum(loss[0]), ('seq', 'head'))  45.5 us

profile of v1, /device:TPU:0, one launch (start us, length us, event | category | flops | bytes accessed | tf_op | source)
XLA Modules:
  0.0 162.9 jit_solution(1135212233938664714)
XLA Ops:
  0.6 0.0 copy-start
  0.6 0.7 copy-done
  1.3 0.6 broadcast_in_dim.2.w_in
  1.9 1.2 copy.5
  3.1 0.3 copy.6
  3.4 0.9 pad.4.u_in
  4.3 107.1 %shard_map.50 = (f32[8,256,128]{2,1,0:T(8,128)}, f32[8,256]{1,0:T(8,128)}) custom-call(bf16[256,2048]{1,0:T(8,128)(2,1)} %bitcast.9, bf16[8,256,128]{2,1,0:T(8,128)(2,1)} %pad.4.u_in, f32[8,256]{1,0:T(8,128)} %broadcast_in_dim.2.w_in), custom_call_target="tpu_custom_call" | custom-call | tf_op jit(solution)/shard_map/pallas_call | solution.py:224
  111.4 1.3 slice_reduce_fusion
  112.8 45.5 %psum.7 = f32[]{:T(128)} all-reduce(f32[]{:T(128)} %slice_reduce_fusion), channel_id=1, replica_groups=mesh['seq'=16,'head'=2] {'seq','head'}, use_global_device_ids=true, to_apply=%region_1.2 | all-reduce | flops 1 | bytes 8 | tf_op jit(solution)/shard_map/psum | solution.py:248
  158.9 1.3 slice_bitcast_fusion
  160.2 0.3 copy.7
  160.5 1.2 copy.8
Async XLA Ops:
  0.6 0.7 copy-start

commit v2 on v1

v2 whole, which is shorter than its diff:
```python
import functools
import math

import jax
import jax.numpy as jnp
from jax import lax
from jax.experimental import pallas as pl
from jax.experimental.pallas import tpu as pltpu
from jax.sharding import PartitionSpec as P

TW = 256
SW = 112
LANES = 128
LOG2E = math.log2(math.e)
LN2 = math.log(2.0)
NT = (((1,), (1,)), ((), ()))


def dot_nt(a, b):
    return lax.dot_general(a, b, NT, preferred_element_type=jnp.float32)


def kernel(
    heads, group, head_shards, t_in, s_in, w_in, grad_out, loss_out,
    u_in, w_tile, t_all, u_all, w_all, state, norms, grads, landed, losses, sums,
    t_send, u_send, w_send, t_fwd, u_fwd, t_recv, u_recv, w_recv, n_send, n_recv, g_send, g_recv,
    l_send, l_recv, s_send, s_recv,
):
    n = heads * group
    block = t_in.shape[0]
    me = lax.axis_index("seq")
    shard = lax.axis_index("head")
    head = lax.div(me, group)
    member = lax.rem(me, group)
    unroll = math.gcd(n, 4)
    t_scale = LOG2E / math.sqrt(TW)
    u_scale = LOG2E / math.sqrt(SW)

    def other_head(i):
        return lax.rem(head + i, heads)

    def source_head(i):
        return lax.rem(head + heads - i, heads)

    def other_member(i):
        return lax.rem(member + i, group)

    def remote(src, dst, send, recv, device):
        target = device if isinstance(device, dict) else {"seq": device}
        return pltpu.make_async_remote_copy(
            src_ref=src, dst_ref=dst, send_sem=send, recv_sem=recv,
            device_id=target, device_id_type=pl.DeviceIdType.MESH,
        )

    def rows(slot):
        return pl.ds(pl.multiple_of(slot * block, block), block)

    def columns(h):
        return pl.ds(pl.multiple_of(h * TW, TW), TW)

    barrier = pltpu.get_barrier_semaphore()
    for i in range(1, n):
        pl.semaphore_signal(barrier, inc=1, device_id={"seq": lax.rem(me + i, n)}, device_id_type=pl.DeviceIdType.MESH)
    for i in range(1, head_shards):
        pl.semaphore_signal(barrier, inc=1, device_id={"head": lax.rem(shard + i, head_shards)}, device_id_type=pl.DeviceIdType.MESH)
    for h in range(heads):
        u_in[h] = jnp.concatenate(
            [s_in[:, h * SW:(h + 1) * SW], jnp.zeros((block, LANES - SW), jnp.bfloat16)], axis=1
        )
    w_tile[...] = jnp.broadcast_to(w_in[...], w_tile.shape)
    pl.semaphore_wait(barrier, n + head_shards - 2)

    direct = []
    for i in range(1, heads):
        h = other_head(i)
        device = h * group + member
        direct += [
            remote(t_in.at[:, columns(h)], t_all.at[rows(me)], t_send.at[i], t_recv.at[me], device),
            remote(u_in.at[h], u_all.at[rows(me)], u_send.at[i], u_recv.at[me], device),
            remote(w_tile, w_all.at[head], w_send.at[i], w_recv.at[head], device),
        ]
    for copy in direct:
        copy.start()

    def forwards(i, slot, t_src, u_src):
        pairs = []
        for g in range(1, group):
            device = head * group + other_member(g)
            pairs += [
                remote(t_src, t_all.at[rows(slot)], t_fwd.at[i, g], t_recv.at[slot], device),
                remote(u_src, u_all.at[rows(slot)], u_fwd.at[i, g], u_recv.at[slot], device),
            ]
        return pairs

    def arrived(slot):
        remote(t_in.at[:, columns(0)], t_all.at[rows(slot)], t_send.at[0], t_recv.at[slot], me).wait_recv()
        remote(u_in.at[0], u_all.at[rows(slot)], u_send.at[0], u_recv.at[slot], me).wait_recv()

    for copy in forwards(0, me, t_in.at[:, columns(head)], u_in.at[head]):
        copy.start()
    t_all[rows(me), :] = t_in[:, columns(head)]
    u_all[rows(me), :] = u_in[head]
    w_all[head] = w_tile[...]

    low = jnp.full((8, block), -1e30, jnp.float32)
    zero = jnp.zeros((8, block), jnp.float32)
    for h in range(heads):
        for k, value in enumerate((low, zero, zero, low, zero)):
            state[h, k] = value

    def tile(row_head, key_head):
        t_own = t_all[rows(row_head * group + member), :]
        u_own = u_all[rows(row_head * group + member), :]
        width = math.gcd(group, 2)

        def step(j, carry):
            t_max, t_sum, t_cross, u_max, u_sum = carry
            for q in range(width):
                keys = rows(key_head * group + j * width + q)
                t_score = (dot_nt(t_all[keys, :], t_own) * t_scale).reshape(block // 8, 8, block)
                u_score = (dot_nt(u_all[keys, :], u_own) * u_scale).reshape(block // 8, 8, block)
                t_top = jnp.maximum(t_max, jnp.max(t_score, axis=0))
                u_top = jnp.maximum(u_max, jnp.max(u_score, axis=0))
                t_exp = jnp.exp2(t_score - t_top[None])
                u_exp = jnp.exp2(u_score - u_top[None])
                t_keep = jnp.exp2(t_max - t_top)
                u_keep = jnp.exp2(u_max - u_top)
                t_sum = t_sum * t_keep + jnp.sum(t_exp, axis=0)
                t_cross = t_cross * t_keep + jnp.sum(t_exp * (t_score - u_score), axis=0)
                u_sum = u_sum * u_keep + jnp.sum(u_exp, axis=0)
                t_max, u_max = t_top, u_top
            return t_max, t_sum, t_cross, u_max, u_sum

        carry = tuple(state[row_head, k] for k in range(5))
        carry = step(0, carry) if group == width else lax.fori_loop(0, group // width, step, carry)
        for k in range(5):
            state[row_head, k] = carry[k]

    def arrival(i, carry):
        h = source_head(i)
        slot = h * group + member

        @pl.when(i > 0)
        def _():
            arrived(slot)
            for copy in forwards(i, slot, t_all.at[rows(slot)], u_all.at[rows(slot)]):
                copy.start()
        for g in range(1, group):
            arrived(h * group + other_member(g))

        def one(j, carry):
            old = j < i
            tile(source_head(jnp.where(old, j, i)), source_head(jnp.where(old, i, j - i)))
            return carry

        return lax.fori_loop(0, 2 * i + 1, one, carry)

    lax.fori_loop(0, heads, arrival, 0)
    for i in range(1, heads):
        remote(w_tile, w_all.at[source_head(i)], w_send.at[0], w_recv.at[source_head(i)], me).wait_recv()

    loss = jnp.zeros((1, block), jnp.float32)
    for i in range(heads):
        t_max, t_sum, t_cross, u_max, u_sum = (state[i, k] for k in range(5))
        t_top = jnp.max(t_max, axis=0, keepdims=True)
        u_top = jnp.max(u_max, axis=0, keepdims=True)
        t_keep = jnp.exp2(t_max - t_top)
        t_total = jnp.sum(t_sum * t_keep, axis=0, keepdims=True)
        t_mixed = jnp.sum(t_cross * t_keep, axis=0, keepdims=True)
        u_total = jnp.sum(u_sum * jnp.exp2(u_max - u_top), axis=0, keepdims=True)
        t_norm = t_top + jnp.log(t_total) * LOG2E
        u_norm = u_top + jnp.log(u_total) * LOG2E
        weight = w_all[i][:1, :]
        weight_log = jnp.log(weight) * LOG2E
        norms[member, i, 0:8, :] = jnp.broadcast_to(t_norm - weight_log, (8, block))
        norms[member, i, 8:16, :] = jnp.broadcast_to(u_norm - weight_log, (8, block))
        loss = loss + weight * (t_mixed / t_total - t_norm + u_norm)
    loss = jnp.sum(loss, axis=1, keepdims=True) * (LN2 / (heads * head_shards * block * n))
    losses[me] = jnp.broadcast_to(loss, losses.shape[1:])
    stats = [
        remote(norms.at[member], norms.at[member], n_send.at[g], n_recv.at[member], head * group + other_member(g))
        for g in range(1, group)
    ]
    for i in range(1, n):
        stats.append(remote(losses.at[me], losses.at[me], l_send.at[i], l_recv.at[me], lax.rem(me + i, n)))
    for copy in stats:
        copy.start()
    for g in range(1, group):
        m = other_member(g)
        remote(norms.at[m], norms.at[m], n_send.at[0], n_recv.at[m], me).wait_recv()

    def row_grad(i):
        slot = i * group + member
        t_own = t_all[rows(slot), :]
        u_own = u_all[rows(slot), :]

        def own_norm(first):
            tall = jnp.broadcast_to(norms[member, i, first:first + 1, :], (LANES, block)).T
            return jnp.concatenate([tall] * (block // LANES), axis=1)

        t_mine = own_norm(0)
        u_mine = own_norm(8)

        def step(j, total):
            for q in range(unroll):
                key = j * unroll + q
                keys = rows(key)
                key_head = lax.div(key, group)
                key_member = lax.rem(key, group)
                t_theirs = norms[key_member, key_head, 0:1, :]
                u_theirs = norms[key_member, key_head, 8:9, :]
                u_keys = u_all[keys, :]
                t_score = dot_nt(t_own, t_all[keys, :]) * t_scale
                u_score = dot_nt(u_own, u_keys) * u_scale
                row_part = jnp.exp2(u_score - u_mine) - jnp.exp2(t_score - t_mine)
                col_part = jnp.exp2(u_score - u_theirs) - jnp.exp2(t_score - t_theirs)
                mix = (row_part + col_part).astype(jnp.bfloat16)
                total = total + jnp.dot(mix, u_keys, preferred_element_type=jnp.float32)
            return total

        total = lax.fori_loop(0, n // unroll, step, jnp.zeros((block, LANES), jnp.float32))
        return total * (1.0 / math.sqrt(SW))

    def send_grad(i, h):
        return remote(grads.at[h], landed.at[head], g_send.at[h], g_recv.at[head], h * group + member)

    def grad_step(i, carry):
        h = other_head(i)
        grads[h] = row_grad(h)
        send_grad(i, h).start()
        return carry

    lax.fori_loop(1, heads, grad_step, 0)
    for i in range(1, n):
        peer = lax.rem(me + i, n)
        remote(losses.at[peer], losses.at[peer], l_send.at[0], l_recv.at[peer], me).wait_recv()
    sums[shard] = jnp.sum(losses[...], axis=0)
    shards = [
        remote(sums.at[shard], sums.at[shard], s_send.at[i], s_recv.at[shard], {"head": lax.rem(shard + i, head_shards)})
        for i in range(1, head_shards)
    ]
    for copy in shards:
        copy.start()
    landed[head] = row_grad(head)
    for i in range(1, head_shards):
        peer = lax.rem(shard + i, head_shards)
        remote(sums.at[peer], sums.at[peer], s_send.at[0], s_recv.at[peer], {"head": peer}).wait_recv()
    loss_out[...] = jnp.sum(sums[...], axis=0)

    for copy in direct + stats + shards:
        copy.wait_send()
    for i in range(heads):
        for copy in forwards(i, me, t_in.at[:, columns(0)], u_in.at[0]):
            copy.wait_send()
    for i in range(1, heads):
        send_grad(i, other_head(i)).wait_send()
    for h in range(heads):
        @pl.when(head != h)
        def _(h=h):
            remote(grads.at[h], landed.at[h], g_send.at[h], g_recv.at[h], me).wait_recv()
        grad_out[:, h * SW:(h + 1) * SW] = landed[h][:, :SW]


def local(teacher, student, weights):
    relations, block, t_columns = teacher.shape
    assert relations == 1
    heads = t_columns // TW
    n = lax.axis_size("seq")
    head_shards = lax.axis_size("head")
    assert n % heads == 0
    group = n // heads
    vmem = pl.BlockSpec(memory_space=pltpu.VMEM)
    dma = pltpu.SemaphoreType.DMA
    student_grad, loss = pl.pallas_call(
        functools.partial(kernel, heads, group, head_shards),
        out_shape=(
            jax.ShapeDtypeStruct((block, heads * SW), jnp.float32),
            jax.ShapeDtypeStruct((8, LANES), jnp.float32),
        ),
        in_specs=[vmem] * 3,
        out_specs=(vmem, vmem),
        scratch_shapes=[
            pltpu.VMEM((heads, block, LANES), jnp.bfloat16),
            pltpu.VMEM((8, block), jnp.float32),
            pltpu.VMEM((n * block, TW), jnp.bfloat16),
            pltpu.VMEM((n * block, LANES), jnp.bfloat16),
            pltpu.VMEM((heads, 8, block), jnp.float32),
            pltpu.VMEM((heads, 5, 8, block), jnp.float32),
            pltpu.VMEM((group, heads, 16, block), jnp.float32),
            pltpu.VMEM((heads, block, LANES), jnp.float32),
            pltpu.VMEM((heads, block, LANES), jnp.float32),
            pltpu.VMEM((n, 8, LANES), jnp.float32),
            pltpu.VMEM((head_shards, 8, LANES), jnp.float32),
            dma((heads,)), dma((heads,)), dma((heads,)),
            dma((heads, group)), dma((heads, group)),
            dma((n,)), dma((n,)), dma((heads,)),
            dma((group,)), dma((group,)),
            dma((heads,)), dma((heads,)),
            dma((n,)), dma((n,)), dma((head_shards,)), dma((head_shards,)),
        ],
        compiler_params=pltpu.CompilerParams(
            collective_id=0, has_side_effects=True, vmem_limit_bytes=60 * 2**20
        ),
    )(teacher[0], student[0], weights[None, :])
    return (loss[0, 0], student_grad[None])


def solution(mesh):
    return jax.shard_map(
        local,
        mesh=mesh,
        in_specs=(P(None, "seq", "head"), P(None, "seq", "head"), P("seq")),
        out_specs=(P(), P(None, "seq", "head")),
        check_vma=False,
    )
```

time: 163 us -> 119 us (0.73)
  the two profiles are of different devices: /device:TPU:0 before, /device:TPU:24 now
where the time goes in v2:
time: 119 us
  Pallas kernels  115 us (97%)
  local copies, waits for them, and re-layouts  3.35 us (3%)
    pallas_call x1, Pallas kernels, local(): pl.pallas_call(functools.partial(kernel, heads, group, head_shards), out_...  115 us

profile of v2, /device:TPU:24, one launch (start us, length us, event | category | flops | bytes accessed | tf_op | source)
XLA Modules:
  0.0 119.1 jit_solution(13106738320246146450)
XLA Ops:
  0.6 115.1 %shard_map.50 = (f32[256,896]{1,0:T(8,128)}, f32[8,128]{1,0:T(8,128)}) custom-call(bf16[256,2048]{1,0:T(8,128)(2,1)} %bitcast.5, bf16[256,896]{1,0:T(8,128)(2,1)} %bitcast.7, f32[1,256]{1,0:T(1,128)} %bitcast.8), custom_call_target="tpu_custom_call" | custom-call | tf_op jit(solution)/shard_map/pallas_call | solution.py:274
  115.8 1.2 slice.3
  117.0 2.2 %copy.6 = f32[1,256,896]{2,1,0:T(8,128)} copy(f32[1,256,896]{2,1,0:T(8,128)} %bitcast.6) | data formatting | bytes 1835008

commit v3 on v2

--- a/solution.py
+++ b/solution.py
@@ -32,7 +32,8 @@
     shard = lax.axis_index("head")
     head = lax.div(me, group)
     member = lax.rem(me, group)
-    unroll = math.gcd(n, 4)
+    unroll = math.gcd(n, 8)
+    pair = math.gcd(heads, 2)
     t_scale = LOG2E / math.sqrt(TW)
     u_scale = LOG2E / math.sqrt(SW)
 
@@ -108,15 +109,16 @@
         for k, value in enumerate((low, zero, zero, low, zero)):
             state[h, k] = value
 
-    def tile(row_head, key_head):
+    def tile(row_head, key_pair):
         t_own = t_all[rows(row_head * group + member), :]
         u_own = u_all[rows(row_head * group + member), :]
         width = math.gcd(group, 2)
+        parts = [(a, q) for a in range(pair) for q in range(width)]
 
         def step(j, carry):
             t_max, t_sum, t_cross, u_max, u_sum = carry
-            for q in range(width):
-                keys = rows(key_head * group + j * width + q)
+            for a, q in parts:
+                keys = rows(source_head(key_pair * pair + a) * group + j * width + q)
                 t_score = (dot_nt(t_all[keys, :], t_own) * t_scale).reshape(block // 8, 8, block)
                 u_score = (dot_nt(u_all[keys, :], u_own) * u_scale).reshape(block // 8, 8, block)
                 t_top = jnp.maximum(t_max, jnp.max(t_score, axis=0))
@@ -136,26 +138,34 @@
         for k in range(5):
             state[row_head, k] = carry[k]
 
-    def arrival(i, carry):
-        h = source_head(i)
-        slot = h * group + member
-
-        @pl.when(i > 0)
-        def _():
-            arrived(slot)
-            for copy in forwards(i, slot, t_all.at[rows(slot)], u_all.at[rows(slot)]):
-                copy.start()
-        for g in range(1, group):
-            arrived(h * group + other_member(g))
+    def arrival(p, carry):
+        for a in range(pair):
+            i = p * pair + a
+            h = source_head(i)
+            slot = h * group + member
+
+            @pl.when(i > 0)
+            def _(i=i, slot=slot):
+                arrived(slot)
+                for copy in forwards(i, slot, t_all.at[rows(slot)], u_all.at[rows(slot)]):
+                    copy.start()
+        for a in range(pair):
+            h = source_head(p * pair + a)
+            for g in range(1, group):
+                arrived(h * group + other_member(g))
 
         def one(j, carry):
-            old = j < i
-            tile(source_head(jnp.where(old, j, i)), source_head(jnp.where(old, i, j - i)))
+            old = j < p * pair
+            fresh = j - p * pair
+            tile(
+                source_head(jnp.where(old, j, p * pair + lax.rem(fresh, pair))),
+                jnp.where(old, p, lax.div(fresh, pair)),
+            )
             return carry
 
-        return lax.fori_loop(0, 2 * i + 1, one, carry)
-
-    lax.fori_loop(0, heads, arrival, 0)
+        return lax.fori_loop(0, p * pair + (p + 1) * pair, one, carry)
+
+    lax.fori_loop(0, heads // pair, arrival, 0)
     for i in range(1, heads):
         remote(w_tile, w_all.at[source_head(i)], w_send.at[0], w_recv.at[source_head(i)], me).wait_recv()
 

time: 119 us -> 111 us (0.933)
  Pallas kernels: 115 us -> 107 us
    pallas_call x1, Pallas kernels: 115 us -> 107 us  [local(): pl.pallas_call(functools.partial(kernel, heads, group, head_shards), out_...]
where the time goes in v3:
time: 111 us
  Pallas kernels  107 us (96%)
  local copies, waits for them, and re-layouts  3.35 us (3%)
    pallas_call x1, Pallas kernels, local(): pl.pallas_call(functools.partial(kernel, heads, group, head_shards), out_...  107 us

profile of v3, /device:TPU:24, one launch (start us, length us, event | category | flops | bytes accessed | tf_op | source)
XLA Modules:
  0.0 110.9 jit_solution(1350009425957316727)
XLA Ops:
  0.6 107.0 %shard_map.50 = (f32[256,896]{1,0:T(8,128)}, f32[8,128]{1,0:T(8,128)}) custom-call(bf16[256,2048]{1,0:T(8,128)(2,1)} %bitcast.5, bf16[256,896]{1,0:T(8,128)(2,1)} %bitcast.7, f32[1,256]{1,0:T(1,128)} %bitcast.8), custom_call_target="tpu_custom_call" | custom-call | tf_op jit(solution)/shard_map/pallas_call | solution.py:284
  107.6 1.2 %slice.3 = f32[1,1]{1,0:T(1,128)} slice(f32[8,128]{1,0:T(8,128)} %get-tuple-element.4), slice={[0:1], [0:1]} | slice | bytes 8 | tf_op jit(solution)/shard_map/slice | solution.py:315
  108.8 2.2 %copy.6 = f32[1,256,896]{2,1,0:T(8,128)} copy(f32[1,256,896]{2,1,0:T(8,128)} %bitcast.6) | data formatting | bytes 1835008
